TPU v7x, 32 devices: a whole 2x2x4 slice. The times are simulated.
32 devices in a mesh: grp: 2 (over y), tile: 4 (over z), coil: 2 (over x), spk: 2 (over core).
Axes of the slice: x: 2, y: 2, z: 4, core: 2. Of those that a mesh axis runs over, the one named last changes fastest.
Arguments:
- coil_maps: float32 [2, 512, 2, 256], P('coil', ('grp', 'tile', 'spk')), parts along dimension 1, may hold values from -6 to 6
- kspace_data: bfloat16 [2, 128, 2, 256], P('coil', ('grp', 'tile', 'spk')), parts along dimension 1, may hold values from -24 to 24
- interp_weights: bfloat16 [128, 6, 256], P(('grp', 'tile', 'spk')), parts along dimension 0, may hold values from 0.099609375 to 1
- sample_bins: int32 [128, 256], P(('grp', 'tile', 'spk')), parts along dimension 0, may hold values from 0 to 65535, as said below
- spoke_count: int32 [16], P(('grp', 'tile', 'spk')), parts along dimension 0, may hold values from 1 to 8, 32 in all
- thresholds: float32 [3], replicated, may hold values from 0.05 to 0.3
Outputs:
- image: float32 [512, 2, 256], P(('grp', 'tile', 'spk')), parts along dimension 0
There are 2 independent parts, one for each index of `grp`. A program takes and returns all parts, laid end to end along the dimension named above; an argument that names none is the same for every part. Nothing has to cross between parts.
Inputs may be any that keep to these rules, and one draw needn't show every extreme that they name: `sample_bins`: sample k of each spoke lies on a straight line through cell (128, 128), at offset k - 128 along the spoke's direction, coordinates taken modulo 256. `spoke_count`: each independent slice has its own 8 counts, and the whole array holds one such block of counts per slice. The 8 counts of each slice sum to 32. In every draw, at least one device of each slice holds 8 live spokes. A device's live spokes are its first ones.
All inputs are finite; a program needn't handle non-finite values.
Results may differ from a plain program's by a relative error of at most 0.0016.
Values may be sent and summed in bfloat16 or wider, within the bound.
A program may use at most 64 MiB of HBM per device.

v0:
```python
import math
import jax
import jax.numpy as jnp
from jax import lax
from jax.sharding import PartitionSpec as P

N = 256
RO = 256
SPK_DEV = 8
LEVELS = 3
ITERS = 4
HIGH = lax.Precision.HIGHEST
STEP_SIZE = 0.5
RSQRT2 = 0.7071067811865476


def dft_table(length, direction):
    positions = jnp.arange(length, dtype=jnp.int32)
    phases = positions[:, None] * positions[None, :] % length
    angles = phases.astype(jnp.float32) * jnp.float32(2.0 * math.pi / length)
    norm_scale = 1.0 / math.sqrt(length)
    cosine = jnp.cos(angles) * norm_scale
    sine_tab = jnp.sin(angles) * norm_scale
    top_rows = jnp.stack([cosine, -direction * sine_tab], axis=1)
    bottom = jnp.stack([direction * sine_tab, cosine], axis=1)
    return jnp.stack([top_rows, bottom], axis=0)


def haar_matrix(length, levels):
    haar_mat = jnp.eye(length, dtype=jnp.float32)
    positions = jnp.arange(length, dtype=jnp.int32)
    out_i = positions[:, None]
    in_j = positions[None, :]
    for level_num in range(levels):
        span_len = length >> level_num
        half_len = span_len // 2
        low_hit = (out_i < half_len) & ((in_j == 2 * out_i) | (in_j == 2 * out_i + 1))
        high_pos = out_i - half_len
        high_hit = (
            (out_i >= half_len)
            & (out_i < span_len)
            & ((in_j == 2 * high_pos) | (in_j == 2 * high_pos + 1))
        )
        sign_val = jnp.where(in_j == 2 * high_pos + 1, -1.0, 1.0)
        step_mat = jnp.where(low_hit, RSQRT2, jnp.where(high_hit, sign_val * RSQRT2, 0.0))
        step_mat = step_mat + jnp.where((out_i >= span_len) & (in_j == out_i), 1.0, 0.0)
        haar_mat = jnp.dot(step_mat.astype(jnp.float32), haar_mat, precision=HIGH)
    return haar_mat


def haar_labels(length, levels):
    positions = jnp.arange(length, dtype=jnp.int32)
    band_label = jnp.ones((length,), jnp.int32)
    for level_num in range(1, levels + 1):
        band_label = band_label + (positions < length >> level_num).astype(jnp.int32)
    return band_label


def wavelet_shrink(target, thresholds, levels):
    row_count, pair_dim, col_count = target.shape
    block_len = 2**levels
    row_haar = haar_matrix(block_len, levels)
    col_haar = haar_matrix(col_count, levels)
    grouped = target.reshape(row_count // block_len, block_len, pair_dim, col_count)
    coeffs = jnp.einsum("ij,gjpc->gipc", row_haar, grouped, precision=HIGH)
    coeffs = jnp.einsum("gipc,kc->gipk", coeffs, col_haar, precision=HIGH)
    band_min = jnp.minimum(
        haar_labels(block_len, levels)[:, None], haar_labels(col_count, levels)[None, :]
    )
    active = band_min <= levels
    limits = jnp.ones(band_min.shape, jnp.float32)
    for level_num in range(levels):
        limits = jnp.where(band_min == level_num + 1, thresholds[level_num], limits)
    magnitude = jnp.sqrt(coeffs[:, :, 0] ** 2 + coeffs[:, :, 1] ** 2)
    factor = jnp.maximum(magnitude - limits, 0.0) / jnp.maximum(magnitude, limits)
    factor = jnp.where(active, factor, 1.0)
    shrunk = coeffs * factor[:, :, None, :]
    restored = jnp.einsum("gipk,kc->gipc", shrunk, col_haar, precision=HIGH)
    restored = jnp.einsum("ij,gipc->gjpc", row_haar, restored, precision=HIGH)
    return restored.reshape(row_count, pair_dim, col_count)


def complex_mul(left, right):
    real_part = left[:, 0] * right[:, 0] - left[:, 1] * right[:, 1]
    imag_part = left[:, 0] * right[:, 1] + left[:, 1] * right[:, 0]
    return jnp.stack([real_part, imag_part], axis=1)


def conj_mul(left, right):
    real_part = left[:, 0] * right[:, 0] + left[:, 1] * right[:, 1]
    imag_part = left[:, 0] * right[:, 1] - left[:, 1] * right[:, 0]
    return jnp.stack([real_part, imag_part], axis=1)


def interp_tables(load_bins, load_interp):
    grid_ids = jnp.arange(N, dtype=jnp.int32)
    row_bins = load_bins // N
    col_bins = load_bins % N
    zero_val = jnp.zeros((), jnp.bfloat16)
    row_table = jnp.zeros((load_bins.shape[0], load_bins.shape[1], N), jnp.bfloat16)
    col_table = jnp.zeros((load_bins.shape[0], N, load_bins.shape[1]), jnp.bfloat16)
    for tap_index in range(3):
        row_hit = grid_ids[None, None, :] == ((row_bins + tap_index - 1) % N)[:, :, None]
        row_table = row_table + jnp.where(
            row_hit, load_interp[:, tap_index, :][:, :, None], zero_val
        )
        col_hit = grid_ids[None, :, None] == ((col_bins + tap_index - 1) % N)[:, None, :]
        col_table = col_table + jnp.where(
            col_hit, load_interp[:, 3 + tap_index, :][:, None, :], zero_val
        )
    return (row_table, col_table)


def local(coil_maps, kspace_data, interp_weights, sample_bins, spoke_count, thresholds):
    blocks = lax.axis_size(("tile", "spk"))
    row_count = coil_maps.shape[1]
    live_total = blocks * SPK_DEV // 2
    coil_sens = coil_maps[0]
    measured = kspace_data[0]
    my_index = lax.axis_index(("tile", "spk"))
    counts = lax.all_gather(spoke_count, ("tile", "spk"), axis=0, tiled=True)
    prefix = jnp.cumsum(counts) - counts
    per_peer = -(-SPK_DEV // blocks)
    peer_ids = jnp.arange(blocks, dtype=jnp.int32)
    first_slot = (peer_ids - prefix[my_index]) % blocks
    slot_index = first_slot[:, None] + blocks * jnp.arange(per_peer, dtype=jnp.int32)[None, :]
    picked = jnp.clip(slot_index, 0, SPK_DEV - 1)
    values = jnp.concatenate([measured, interp_weights], axis=1)
    got_values = lax.all_to_all(
        values[picked], ("tile", "spk"), split_axis=0, concat_axis=0, tiled=True
    )
    got_bins = lax.all_to_all(
        sample_bins[picked], ("tile", "spk"), split_axis=0, concat_axis=0, tiled=True
    )
    my_share = SPK_DEV // 2
    wanted = my_index + blocks * jnp.arange(my_share, dtype=jnp.int32)
    source = jnp.sum((prefix[None, :] <= wanted[:, None]).astype(jnp.int32), axis=1) - 1
    depth_at = (wanted - prefix[source]) // blocks
    loaded = got_values[source, depth_at]
    load_bins = got_bins[source, depth_at]
    load_data = loaded[:, 0:2]
    load_interp = loaded[:, 2:8]
    row_table, col_table = interp_tables(load_bins, load_interp)
    n_load = row_table.shape[0]
    offset = jnp.abs(jnp.arange(RO, dtype=jnp.int32) - RO // 2).astype(jnp.float32)
    density = (offset + 0.5) * (N / (3.0 * RO * live_total))
    target_data = load_data.astype(jnp.float32)
    fwd_table = dft_table(N, 1.0)
    inv_table = dft_table(N, -1.0)

    def grid_rows(weighted):

        def grid_term(row_start, piece_rows):

            def grid_one_spoke(spoke_index, partial_value):
                row_one = lax.dynamic_index_in_dim(row_table, spoke_index, 0, keepdims=False)
                col_one = lax.dynamic_index_in_dim(col_table, spoke_index, 0, keepdims=False)
                col_slice = col_one.astype(jnp.float32)
                residue = lax.dynamic_index_in_dim(weighted, spoke_index, 0, keepdims=False)
                smeared = (col_slice[:, None, :] * residue[None, :, :]).astype(jnp.bfloat16)
                added = jnp.dot(
                    smeared.reshape(piece_rows * 2, RO), row_one, preferred_element_type=jnp.float32
                )
                return partial_value + added.reshape(piece_rows, 2, N)

            return lax.fori_loop(
                0, my_share, grid_one_spoke, jnp.zeros((piece_rows, 2, N), jnp.float32)
            )

        return grid_term

    estimate = jnp.zeros((row_count, 2, N), jnp.float32)
    for iteration in range(ITERS):
        if iteration == 0:
            weighted = -density[None, None, :] * target_data
        else:
            coil_image = complex_mul(coil_sens, estimate)
            half_done = jnp.einsum("rpc,pcqv->rqv", coil_image, fwd_table, precision=HIGH)
            turned = lax.all_to_all(
                half_done, ("tile", "spk"), split_axis=2, concat_axis=0, tiled=True
            )
            kspace = jnp.einsum("rpv,prqu->vqu", turned, fwd_table, precision=HIGH).astype(
                jnp.bfloat16
            )
            piece = lax.all_gather(kspace, ("tile", "spk"), axis=0, tiled=True)
            fold_piece_rows = piece.shape[0]
            flat_piece = piece.reshape(fold_piece_rows * 2, N)

            def fold_one_spoke(spoke_index, partial_value):
                row_one = lax.dynamic_index_in_dim(row_table, spoke_index, 0, keepdims=False)
                col_one = lax.dynamic_index_in_dim(col_table, spoke_index, 0, keepdims=False)
                inner_sum = lax.dot_general(
                    flat_piece,
                    row_one,
                    (((1,), (1,)), ((), ())),
                    preferred_element_type=jnp.float32,
                )
                inner_sum = inner_sum.reshape(fold_piece_rows, 2, RO)
                col_slice = col_one.astype(jnp.float32)
                added = jnp.sum(inner_sum * col_slice[:, None, :], axis=0)
                current = lax.dynamic_index_in_dim(partial_value, spoke_index, 0, keepdims=False)
                return lax.dynamic_update_index_in_dim(
                    partial_value, current + added, spoke_index, 0
                )

            sample_model = lax.fori_loop(
                0, my_share, fold_one_spoke, jnp.zeros((n_load, 2, RO), jnp.float32)
            )
            weighted = density[None, None, :] * (sample_model - target_data)
        grid_term = grid_rows(weighted)
        owned_rows = lax.psum_scatter(
            grid_term(jnp.int32(0), row_count * lax.axis_size(("tile", "spk"))),
            ("tile", "spk"),
            scatter_dimension=0,
            tiled=True,
        )
        partial_back = jnp.einsum("vpu,puqr->vqr", owned_rows, inv_table, precision=HIGH)
        returned = lax.all_to_all(
            partial_back, ("tile", "spk"), split_axis=2, concat_axis=0, tiled=True
        )
        coil_back = jnp.einsum("vpr,pvqc->rqc", returned, inv_table, precision=HIGH)
        gradient = lax.psum(conj_mul(coil_sens, coil_back), "coil")
        estimate = wavelet_shrink(estimate - STEP_SIZE * gradient, thresholds, LEVELS)
    return estimate


def solution(mesh):
    placed = (
        P("coil", ("grp", "tile", "spk"), None, None),
        P("coil", ("grp", "tile", "spk"), None, None),
        P(("grp", "tile", "spk"), None, None),
        P(("grp", "tile", "spk"), None),
        P(("grp", "tile", "spk")),
        P(),
    )
    return jax.shard_map(
        local,
        mesh=mesh,
        in_specs=placed,
        out_specs=P(("grp", "tile", "spk"), None, None),
        check_vma=False,
    )
```

profile of v0, /device:TPU:0, one launch (start us, length us, event | category | flops | bytes accessed | tf_op | source)
XLA Modules:
  0.0 512.3 jit_solution(6684872715194408570)
XLA Ops:
  9.2 10.6 %all-reduce = s32[8]{0:T(128)S(1)} all-reduce(s32[8]{0:T(128)S(1)} %dynamic-update-slice), channel_id=1, replica_groups=mesh['grp'=2,'tile'=4,'coil'=2,'spk'=2] {'tile','spk'}, use_global_device_ids=true, to_apply=%add | all-reduce | flops 8 | bytes 64
  22.5 3.3 all-to-all-start
  34.2 5.0 all-to-all-start.1
  39.9 5.1 all-to-all-done.1
  47.7 7.5 %while.98 = (s32[]{:T(128)}, f32[256,2,256]{2,0,1:T(8,128)}, bf16[4,256,256]{2,1,0:T(8,128)(2,1)S(1)}, f32[4,2,256]{2,1,0:T(2,128)S(1)}, bf16[4,256,256]{2,1,0:T(8,128)(2,1)S(1)}, /*index=5*/s32[]{:T(128)}, s32[]{:T(128)}) while((s32[]{:T(128)}, f32[256,2,256]{2,0,1:T(8,128)}, bf16[4,256,256]{2,1,0:T(8,128)(2,1)S(1)}, ...), condition=%wide.region_3.4_spmd.clone, body=%wide.region_2.3_spmd.clone.sunk | while | flops 67698688 | bytes 1841251 | solution.py:166
  48.8 2.1 convolution_add_fusion.8
  51.0 2.1 convolution_add_fusion.8
  53.1 2.1 convolution_add_fusion.8
  57.0 2.7 select_select_fusion
  60.5 24.4 %reduce-scatter.5.cloned.1.call-done = f32[32,2,256]{2,0,1:T(8,128)} async-done(((f32[256,2,256]{2,0,1:T(8,128)}), f32[32,2,256]{2,0,1:T(8,128)}) %reduce-scatter.5.cloned.1.call-update) | async-done | bytes 65552 | tf_op jit(solution)/shard_map/reduce_scatter | solution.py:211
  89.2 3.4 all-to-all-start.2
  94.6 3.8 all-to-all-done.2
  107.4 18.6 %all-reduce.6.cloned.1.call-done = f32[32,2,256]{2,0,1:T(8,128)} async-done(((f32[32,2,256]{2,0,1:T(8,128)}), f32[32,2,256]{2,0,1:T(8,128)}) %all-reduce.6.cloned.1.call-update) | async-done | bytes 65552 | tf_op jit(solution)/shard_map/psum | solution.py:222
  133.2 4.6 all-to-all-start.3
  138.6 5.2 %all-to-all-done.3 = f32[8,1,2048]{2,1,0:T(1,128)} async-done(((f32[8,1,2048]{2,1,0:T(1,128)}), f32[8,1,2048]{2,1,0:T(1,128)}, u32[]{:S(2)}, u32[]{:S(2)}) %all-to-all-start.3) | async-done | bytes 65568 | tf_op jit(solution)/shard_map/all_to_all | solution.py:179
  143.8 2.2 reduce.1
  152.9 14.2 %all_gather.13 = bf16[256,2,256]{2,0,1:T(8,128)(2,1)S(1)} all-gather(bf16[32,2,256]{2,0,1:T(8,128)(2,1)S(1)} %fusion.32), channel_id=1, replica_groups=mesh['grp'=2,'tile'=4,'coil'=2,'spk'=2] {'tile','spk'}, dimensions={0}, use_global_device_ids=true | all-gather | bytes 294912 | tf_op jit(solution)/shard_map/all_gather | solution.py:185
  168.1 12.7 %while.95 = (s32[]{:T(128)}, f32[4,2,256]{2,1,0:T(2,128)}, bf16[4,256,256]{2,1,0:T(8,128)(2,1)S(1)}, bf16[512,256]{1,0:T(8,128)(2,1)S(1)}, bf16[4,256,256]{2,1,0:T(8,128)(2,1)S(1)}, /*index=5*/s32[]{:T(128)}) while((s32[]{:T(128)}, f32[4,2,256]{2,1,0:T(2,128)}, bf16[4,256,256]{2,1,0:T(8,128)(2,1)S(1)}, bf16[512,256]{1,0:T(8,128)(2,1)S(1)}, ...), condition=%wide.region_8.9_spmd, body=%wide.region_6.8_spmd.sunk | while | flops 67436544 | bytes 6300293 | solution.py:206
  182.3 7.5 %while.99 = (s32[]{:T(128)}, f32[256,2,256]{2,0,1:T(8,128)}, bf16[4,256,256]{2,1,0:T(8,128)(2,1)S(1)}, f32[4,2,256]{2,1,0:T(2,128)S(1)}, bf16[4,256,256]{2,1,0:T(8,128)(2,1)S(1)}, /*index=5*/s32[]{:T(128)}, s32[]{:T(128)}) while((s32[]{:T(128)}, f32[256,2,256]{2,0,1:T(8,128)}, bf16[4,256,256]{2,1,0:T(8,128)(2,1)S(1)}, ...), condition=%wide.region_10.11_spmd.clone, body=%wide.region_9.10_spmd.clone.sunk | while | flops 67698688 | bytes 1841251 | solution.py:166
  183.4 2.1 convolution_add_fusion.9
  185.5 2.1 convolution_add_fusion.9
  187.6 2.1 convolution_add_fusion.9
  189.8 28.9 %reduce-scatter.7.cloned.1.call-done = f32[32,2,256]{2,0,1:T(8,128)} async-done(((f32[256,2,256]{2,0,1:T(8,128)}), f32[32,2,256]{2,0,1:T(8,128)}) %reduce-scatter.7.cloned.1.call-update) | async-done | bytes 65552 | tf_op jit(solution)/shard_map/reduce_scatter | solution.py:211
  220.7 8.3 %all_to_all.136 = f32[8,1,2048]{2,1,0:T(1,128)S(1)} all-to-all(f32[8,1,2048]{2,1,0:T(1,128)S(1)} %reshape.884), channel_id=1, replica_groups=mesh['grp'=2,'tile'=4,'coil'=2,'spk'=2] {'tile','spk'}, dimensions={0} | all-to-all | bytes 131072 | tf_op jit(solution)/shard_map/all_to_all | solution.py:218
  231.7 19.7 %all-reduce.8.cloned.1.call-done = f32[32,2,256]{2,0,1:T(8,128)} async-done(((f32[32,2,256]{2,0,1:T(8,128)}), f32[32,2,256]{2,0,1:T(8,128)}) %all-reduce.8.cloned.1.call-update) | async-done | bytes 65552 | tf_op jit(solution)/shard_map/psum | solution.py:222
  258.9 4.6 all-to-all-start.5
  263.5 6.0 %all-to-all-done.5 = f32[8,1,2048]{2,1,0:T(1,128)} async-done(((f32[8,1,2048]{2,1,0:T(1,128)}), f32[8,1,2048]{2,1,0:T(1,128)}, u32[]{:S(2)}, u32[]{:S(2)}) %all-to-all-start.5) | async-done | bytes 65568 | tf_op jit(solution)/shard_map/all_to_all | solution.py:179
  269.5 2.2 reduce.3
  278.6 14.2 %all_gather.14 = bf16[256,2,256]{2,0,1:T(8,128)(2,1)S(1)} all-gather(bf16[32,2,256]{2,0,1:T(8,128)(2,1)S(1)} %fusion.33), channel_id=1, replica_groups=mesh['grp'=2,'tile'=4,'coil'=2,'spk'=2] {'tile','spk'}, dimensions={0}, use_global_device_ids=true | all-gather | bytes 294912 | tf_op jit(solution)/shard_map/all_gather | solution.py:185
  293.8 12.7 %while.96 = (s32[]{:T(128)}, f32[4,2,256]{2,1,0:T(2,128)}, bf16[4,256,256]{2,1,0:T(8,128)(2,1)S(1)}, bf16[512,256]{1,0:T(8,128)(2,1)S(1)}, bf16[4,256,256]{2,1,0:T(8,128)(2,1)S(1)}, /*index=5*/s32[]{:T(128)}) while((s32[]{:T(128)}, f32[4,2,256]{2,1,0:T(2,128)}, bf16[4,256,256]{2,1,0:T(8,128)(2,1)S(1)}, bf16[512,256]{1,0:T(8,128)(2,1)S(1)}, ...), condition=%wide.region_15.16_spmd, body=%wide.region_13.15_spmd.sunk | while | flops 67436544 | bytes 6300293 | solution.py:206
  307.9 7.5 %while.100 = (s32[]{:T(128)}, f32[256,2,256]{2,0,1:T(8,128)}, bf16[4,256,256]{2,1,0:T(8,128)(2,1)S(1)}, f32[4,2,256]{2,1,0:T(2,128)S(1)}, bf16[4,256,256]{2,1,0:T(8,128)(2,1)S(1)}, /*index=5*/s32[]{:T(128)}, s32[]{:T(128)}) while((s32[]{:T(128)}, f32[256,2,256]{2,0,1:T(8,128)}, bf16[4,256,256]{2,1,0:T(8,128)(2,1)S(1)}, ...), condition=%wide.region_17.18_spmd.clone, body=%wide.region_16.17_spmd.clone.sunk | while | flops 67698688 | bytes 1841251 | solution.py:166
  309.0 2.1 convolution_add_fusion.10
  311.1 2.1 convolution_add_fusion.10
  315.6 28.8 %reduce-scatter.9.cloned.1.call-done = f32[32,2,256]{2,0,1:T(8,128)} async-done(((f32[256,2,256]{2,0,1:T(8,128)}), f32[32,2,256]{2,0,1:T(8,128)}) %reduce-scatter.9.cloned.1.call-update) | async-done | bytes 65552 | tf_op jit(solution)/shard_map/reduce_scatter | solution.py:211
  346.4 8.3 %all_to_all.137 = f32[8,1,2048]{2,1,0:T(1,128)S(1)} all-to-all(f32[8,1,2048]{2,1,0:T(1,128)S(1)} %reshape.888), channel_id=1, replica_groups=mesh['grp'=2,'tile'=4,'coil'=2,'spk'=2] {'tile','spk'}, dimensions={0} | all-to-all | bytes 131072 | tf_op jit(solution)/shard_map/all_to_all | solution.py:218
  357.4 19.5 %all-reduce.10.cloned.1.call-done = f32[32,2,256]{2,0,1:T(8,128)} async-done(((f32[32,2,256]{2,0,1:T(8,128)}), f32[32,2,256]{2,0,1:T(8,128)}) %all-reduce.10.cloned.1.call-update) | async-done | bytes 65552 | tf_op jit(solution)/shard_map/psum | solution.py:222
  384.4 4.6 all-to-all-start.7
  389.0 6.0 %all-to-all-done.7 = f32[8,1,2048]{2,1,0:T(1,128)} async-done(((f32[8,1,2048]{2,1,0:T(1,128)}), f32[8,1,2048]{2,1,0:T(1,128)}, u32[]{:S(2)}, u32[]{:S(2)}) %all-to-all-start.7) | async-done | bytes 65568 | tf_op jit(solution)/shard_map/all_to_all | solution.py:179
  395.0 2.2 reduce.5
  404.1 14.2 %all_gather.15 = bf16[256,2,256]{2,0,1:T(8,128)(2,1)S(1)} all-gather(bf16[32,2,256]{2,0,1:T(8,128)(2,1)S(1)} %fusion.34), channel_id=1, replica_groups=mesh['grp'=2,'tile'=4,'coil'=2,'spk'=2] {'tile','spk'}, dimensions={0}, use_global_device_ids=true | all-gather | bytes 294912 | tf_op jit(solution)/shard_map/all_gather | solution.py:185
  419.3 12.7 %while.97 = (s32[]{:T(128)}, f32[4,2,256]{2,1,0:T(2,128)}, bf16[4,256,256]{2,1,0:T(8,128)(2,1)S(1)}, bf16[512,256]{1,0:T(8,128)(2,1)S(1)}, bf16[4,256,256]{2,1,0:T(8,128)(2,1)S(1)}, /*index=5*/s32[]{:T(128)}) while((s32[]{:T(128)}, f32[4,2,256]{2,1,0:T(2,128)}, bf16[4,256,256]{2,1,0:T(8,128)(2,1)S(1)}, bf16[512,256]{1,0:T(8,128)(2,1)S(1)}, ...), condition=%wide.region_22.23_spmd, body=%wide.region_20.22_spmd.sunk | while | flops 67436544 | bytes 6300293 | solution.py:206
  433.5 7.5 %while.101 = (s32[]{:T(128)}, f32[256,2,256]{2,0,1:T(8,128)}, bf16[4,256,256]{2,1,0:T(8,128)(2,1)S(1)}, f32[4,2,256]{2,1,0:T(2,128)S(1)}, bf16[4,256,256]{2,1,0:T(8,128)(2,1)S(1)}, /*index=5*/s32[]{:T(128)}, s32[]{:T(128)}) while((s32[]{:T(128)}, f32[256,2,256]{2,0,1:T(8,128)}, bf16[4,256,256]{2,1,0:T(8,128)(2,1)S(1)}, ...), condition=%wide.region_24.25_spmd.clone, body=%wide.region_23.24_spmd.clone.sunk | while | flops 67698688 | bytes 1841251 | solution.py:166
  434.6 2.1 convolution_add_fusion.11
  436.7 2.1 convolution_add_fusion.11
  438.9 2.1 convolution_add_fusion.11
  441.0 28.9 %reduce-scatter.11.cloned.1.call-done = f32[32,2,256]{2,0,1:T(8,128)} async-done(((f32[256,2,256]{2,0,1:T(8,128)}), f32[32,2,256]{2,0,1:T(8,128)}) %reduce-scatter.11.cloned.1.call-update) | async-done | bytes 65552 | tf_op jit(solution)/shard_map/reduce_scatter | solution.py:211
  472.0 8.3 %all_to_all.138 = f32[8,1,2048]{2,1,0:T(1,128)S(1)} all-to-all(f32[8,1,2048]{2,1,0:T(1,128)S(1)} %reshape.892), channel_id=1, replica_groups=mesh['grp'=2,'tile'=4,'coil'=2,'spk'=2] {'tile','spk'}, dimensions={0} | all-to-all | bytes 131072 | tf_op jit(solution)/shard_map/all_to_all | solution.py:218
  483.0 19.5 %all-reduce.12.cloned.1.call-done = f32[32,2,256]{2,0,1:T(8,128)} async-done(((f32[32,2,256]{2,0,1:T(8,128)}), f32[32,2,256]{2,0,1:T(8,128)}) %all-reduce.12.cloned.1.call-update) | async-done | bytes 65552 | tf_op jit(solution)/shard_map/psum | solution.py:222
  (406 shorter events, 145.9 us)
Async XLA Ops:
  6.5 14.8 %copy-start = (s32[8,256]{1,0:T(8,128)S(1)}, s32[8,256]{1,0:T(8,128)}, u32[]{:S(2)}) copy-start(s32[8,256]{1,0:T(8,128)} %param.23) | copy-start | bytes 24580
  22.5 11.7 %all-to-all-start = ((s32[8,1,256]{2,1,0:T(1,128)}), s32[8,1,256]{2,1,0:T(1,128)S(1)}, u32[]{:S(2)}, u32[]{:S(2)}) async-start(s32[8,1,256]{2,1,0:T(1,128)} %copy.115), calls=%async_computation | async-start | bytes 16384 | tf_op jit(solution)/shard_map/all_to_all | solution.py:132
  27.9 31.9 %copy-start.26 = (s32[8]{0:T(128)}, s32[8]{0:T(128)S(1)}, u32[]{:S(2)}) copy-start(s32[8]{0:T(128)S(1)} %get-tuple-element.881) | copy-start | bytes 100
  27.9 31.9 %copy-start.28 = (s32[8]{0:T(128)}, s32[8]{0:T(128)S(1)}, u32[]{:S(2)}) copy-start(s32[8]{0:T(128)S(1)} %get-tuple-element.882) | copy-start | bytes 100
  28.9 0.7 copy-start.19
  29.7 1.3 copy-start.23
  31.2 120.2 %copy-start.1 = (f32[1,256,2,256]{3,1,2,0:T(8,128)}, f32[1,256,2,256]{3,1,2,0:T(8,128)S(1)}, u32[]{:S(2)}) copy-start(f32[1,256,2,256]{3,1,2,0:T(8,128)S(1)} %get-tuple-element.830) | copy-start | bytes 1572868
  31.2 120.2 %copy-start.4 = (f32[1,256,2,256]{3,1,2,0:T(8,128)}, f32[1,256,2,256]{3,1,2,0:T(8,128)S(1)}, u32[]{:S(2)}) copy-start(f32[1,256,2,256]{3,1,2,0:T(8,128)S(1)} %get-tuple-element.833) | copy-start | bytes 1572868
  34.2 10.8 %all-to-all-start.1 = ((bf16[8,1,8,256]{3,2,1,0:T(8,128)(2,1)}), bf16[8,1,8,256]{3,2,1,0:T(8,128)(2,1)S(1)}, u32[]{:S(2)}, u32[]{:S(2)}) async-start(bf16[8,1,8,256]{3,2,1,0:T(8,128)(2,1)} %bitcast.26), calls=%async_computation.1 | async-start | bytes 65536 | tf_op jit(solution)/shard_map/all_to_all | solution.py:129
  39.2 45.7 %reduce-scatter.5.cloned.1.call-start = ((), (), s32[]{:S(2)}) async-start(), calls=%async_computation.13 | async-start | bytes 589824 | tf_op jit(solution)/shard_map/reduce_scatter | solution.py:211
  89.2 9.2 %all-to-all-start.2 = ((f32[8,1,2048]{2,1,0:T(1,128)}), f32[8,1,2048]{2,1,0:T(1,128)S(1)}, u32[]{:S(2)}, u32[]{:S(2)}) async-start(f32[8,1,2048]{2,1,0:T(1,128)} %reshape.880), calls=%async_computation.3 | async-start | bytes 131072 | tf_op jit(solution)/shard_map/all_to_all | solution.py:218
  92.6 33.5 %all-reduce.6.cloned.1.call-start = ((), (), s32[]{:S(2)}) async-start(), calls=%async_computation.14 | async-start | bytes 131072 | tf_op jit(solution)/shard_map/psum | solution.py:222
  105.8 0.7 copy-start.31
  133.2 10.6 %all-to-all-start.3 = ((f32[8,1,2048]{2,1,0:T(1,128)}), f32[8,1,2048]{2,1,0:T(1,128)}, u32[]{:S(2)}, u32[]{:S(2)}) async-start(f32[8,1,2048]{2,1,0:T(1,128)} %reshape.882), calls=%async_computation.4 | async-start | bytes 131072 | tf_op jit(solution)/shard_map/all_to_all | solution.py:179
  137.8 80.9 %reduce-scatter.7.cloned.1.call-start = ((), (), s32[]{:S(2)}) async-start(), calls=%async_computation.15 | async-start | bytes 589824 | tf_op jit(solution)/shard_map/reduce_scatter | solution.py:211
  169.7 1.6 copy-start.10
  171.3 0.7 copy-start.9
  172.8 1.6 copy-start.10
  174.5 0.7 copy-start.9
  176.0 1.6 copy-start.10
  177.7 0.7 copy-start.9
  179.2 1.6 copy-start.10
  189.7 61.7 %all-reduce.8.cloned.1.call-start = ((), (), s32[]{:S(2)}) async-start(), calls=%async_computation.16 | async-start | bytes 131072 | tf_op jit(solution)/shard_map/psum | solution.py:222
  251.5 1.4 copy-start.15
  252.5 1.0 copy-start.5
  252.9 1.1 copy-start.2
  258.9 10.6 %all-to-all-start.5 = ((f32[8,1,2048]{2,1,0:T(1,128)}), f32[8,1,2048]{2,1,0:T(1,128)}, u32[]{:S(2)}, u32[]{:S(2)}) async-start(f32[8,1,2048]{2,1,0:T(1,128)} %reshape.886), calls=%async_computation.7 | async-start | bytes 131072 | tf_op jit(solution)/shard_map/all_to_all | solution.py:179
  263.5 81.0 %reduce-scatter.9.cloned.1.call-start = ((), (), s32[]{:S(2)}) async-start(), calls=%async_computation.17 | async-start | bytes 589824 | tf_op jit(solution)/shard_map/reduce_scatter | solution.py:211
  295.3 1.6 copy-start.12
  296.9 0.7 copy-start.11
  298.5 1.6 copy-start.12
  301.6 1.6 copy-start.12
  304.8 1.6 copy-start.12
  315.4 61.6 %all-reduce.10.cloned.1.call-start = ((), (), s32[]{:S(2)}) async-start(), calls=%async_computation.18 | async-start | bytes 131072 | tf_op jit(solution)/shard_map/psum | solution.py:222
  377.0 1.4 copy-start.16
  378.0 1.0 copy-start.6
  378.4 1.1 copy-start.3
  384.4 10.6 %all-to-all-start.7 = ((f32[8,1,2048]{2,1,0:T(1,128)}), f32[8,1,2048]{2,1,0:T(1,128)}, u32[]{:S(2)}, u32[]{:S(2)}) async-start(f32[8,1,2048]{2,1,0:T(1,128)} %reshape.890), calls=%async_computation.10 | async-start | bytes 131072 | tf_op jit(solution)/shard_map/all_to_all | solution.py:179
  389.0 81.0 %reduce-scatter.11.cloned.1.call-start = ((), (), s32[]{:S(2)}) async-start(), calls=%async_computation.19 | async-start | bytes 589824 | tf_op jit(solution)/shard_map/reduce_scatter | solution.py:211
  419.3 0.7 copy-start.7
  420.9 1.6 copy-start.8
  422.5 0.7 copy-start.7
  424.0 1.6 copy-start.8
  425.7 0.7 copy-start.7
  427.2 1.6 copy-start.8
  428.9 0.7 copy-start.7
  430.4 1.6 copy-start.8
  441.0 61.5 %all-reduce.12.cloned.1.call-start = ((), (), s32[]{:S(2)}) async-start(), calls=%async_computation.20 | async-start | bytes 131072 | tf_op jit(solution)/shard_map/psum | solution.py:222
  (20 other events, 13.5 us)
Sparse Core Ops, SparseCore 0:
  55.3 29.5 reduce-scatter.4
  106.6 19.3 all-reduce.5
  189.9 28.8 reduce-scatter.6
  231.9 19.5 all-reduce.7
  315.5 28.9 reduce-scatter.8
  357.6 19.3 all-reduce.9
  441.1 28.8 reduce-scatter.10
  483.1 19.3 all-reduce.11
where the time goes:
time: 516 us; the launch traced here: 512 us
  waiting for transfers between devices  215 us (42%)
  blocking collectives  78.2 us (15%)
  local copies, waits for them, and re-layouts  69.4 us (13%)
  matrix products  62 us (12%)
  other arithmetic  46.1 us (9%)
  starting transfers between devices  26.2 us (5%)
  between operations  15.1 us (3%)
    reduce_scatter x4, waiting for transfers between devices, local(): lax.psum_scatter(grid_term(jnp.int32(0), row_count * lax.axis_size(('tile...  111 us
    psum x4, waiting for transfers between devices, local(): gradient = lax.psum(conj_mul(coil_sens, coil_back), 'coil')  77.4 us
    all_gather x3, blocking collectives, local(): piece = lax.all_gather(kspace, ('tile', 'spk'), axis=0, tiled=True)  42.6 us
    dot_general x16, matrix products, grid_one_spoke(): jnp.dot(smeared.reshape(piece_rows * 2, RO), row_one, preferred_element_t...  29.2 us
    all_to_all x3, blocking collectives, local(): lax.all_to_all(partial_back, ('tile', 'spk'), split_axis=2, concat_axis=0...  24.9 us
    unnamed x82, local copies, waits for them, and re-layouts  24.4 us
    all_to_all x3, waiting for transfers between devices, local(): lax.all_to_all(half_done, ('tile', 'spk'), split_axis=2, concat_axis=0, t...  17.1 us
    dynamic_update_slice x12, other arithmetic, fold_one_spoke(): lax.dynamic_update_index_in_dim(partial_value, current + added, spoke_ind...  15.1 us
  transfers between devices with their start and end apart: 14, of which 13 were waited for; matrix products, arithmetic and copies ran while one was open for 3% of the time, Pallas kernels for 0%

commit v1 on v0

--- a/solution.py
+++ b/solution.py
@@ -219,7 +219,9 @@
             partial_back, ("tile", "spk"), split_axis=2, concat_axis=0, tiled=True
         )
         coil_back = jnp.einsum("vpr,pvqc->rqc", returned, inv_table, precision=HIGH)
-        gradient = lax.psum(conj_mul(coil_sens, coil_back), "coil")
+        x = conj_mul(coil_sens, coil_back)
+        pieces = lax.all_gather(x, "coil")
+        gradient = jnp.sum(pieces, axis=0)
         estimate = wavelet_shrink(estimate - STEP_SIZE * gradient, thresholds, LEVELS)
     return estimate
 

time: 516 us -> 463 us (0.90)
  waiting for transfers between devices: 215 us -> 139 us
  blocking collectives: 78.2 us -> 98.3 us
  matrix products: 62 us -> 70.9 us
    psum x4 -> x0, waiting for transfers between devices: 77.4 us -> none  [local(): gradient = lax.psum(conj_mul(coil_sens, coil_back), 'coil')]
    all_gather x0 -> x4, blocking collectives: none -> 19.8 us  [local(): pieces = lax.all_gather(x, 'coil')]
    dot_general x12, matrix products: 3.06 us -> 14.5 us  [fold_one_spoke(): lax.dot_general(flat_piece, row_one, (((1,), (1,)), ((), ())), preferred_...]
    while x48 -> x0, local copies, waits for them, and re-layouts: 8.62 us -> none
    unnamed x82 -> x88, local copies, waits for them, and re-layouts: 24.4 us -> 25.8 us
  transfers between devices with their start and end apart: 14 -> 10, of which waited for: 13 -> 9; matrix products, arithmetic and copies ran while one was open for 3% -> 4% of each run, Pallas kernels for 0% -> 0%
where the time goes in v1:
time: 463 us; the launch traced here: 459 us
  waiting for transfers between devices  139 us (30%)
  blocking collectives  98.3 us (21%)
  matrix products  70.9 us (15%)
  local copies, waits for them, and re-layouts  64.3 us (14%)
  other arithmetic  47.4 us (10%)
  starting transfers between devices  23.9 us (5%)
  between operations  14.7 us (3%)
    reduce_scatter x4, waiting for transfers between devices, local(): lax.psum_scatter(grid_term(jnp.int32(0), row_count * lax.axis_size(('tile...  112 us
    all_gather x3, blocking collectives, local(): piece = lax.all_gather(kspace, ('tile', 'spk'), axis=0, tiled=True)  42.9 us
    dot_general x16, matrix products, grid_one_spoke(): jnp.dot(smeared.reshape(piece_rows * 2, RO), row_one, preferred_element_t...  29.3 us
    unnamed x88, local copies, waits for them, and re-layouts  25.8 us
    all_to_all x3, blocking collectives, local(): lax.all_to_all(partial_back, ('tile', 'spk'), split_axis=2, concat_axis=0...  24.9 us
    all_gather x4, blocking collectives, local(): pieces = lax.all_gather(x, 'coil')  19.8 us
    all_to_all x3, waiting for transfers between devices, local(): lax.all_to_all(half_done, ('tile', 'spk'), split_axis=2, concat_axis=0, t...  16.8 us
    dynamic_update_slice x12, other arithmetic, fold_one_spoke(): lax.dynamic_update_index_in_dim(partial_value, current + added, spoke_ind...  15.1 us
  transfers between devices with their start and end apart: 10, of which 9 were waited for; matrix products, arithmetic and copies ran while one was open for 4% of the time, Pallas kernels for 0%

profile of v1, /device:TPU:0, one launch (start us, length us, event | category | flops | bytes accessed | tf_op | source)
XLA Modules:
  0.0 458.7 jit_solution(15881640661366813184)
XLA Ops:
  9.2 10.6 %all-reduce = s32[8]{0:T(128)S(1)} all-reduce(s32[8]{0:T(128)S(1)} %dynamic-update-slice), channel_id=1, replica_groups=mesh['grp'=2,'tile'=4,'coil'=2,'spk'=2] {'tile','spk'}, use_global_device_ids=true, to_apply=%add | all-reduce | flops 8 | bytes 64
  22.5 3.3 all-to-all-start
  38.0 5.0 %all-to-all-start.1 = ((bf16[8,1,8,256]{3,2,1,0:T(8,128)(2,1)}), bf16[8,1,8,256]{3,2,1,0:T(8,128)(2,1)S(1)}, u32[]{:S(2)}, u32[]{:S(2)}) async-start(bf16[8,1,8,256]{3,2,1,0:T(8,128)(2,1)} %bitcast.26), calls=%async_computation.1 | async-start | bytes 65536 | tf_op jit(solution)/shard_map/all_to_all | solution.py:129
  43.7 5.1 %all-to-all-done.1 = bf16[8,1,8,256]{3,2,1,0:T(8,128)(2,1)S(1)} async-done(((bf16[8,1,8,256]{3,2,1,0:T(8,128)(2,1)}), bf16[8,1,8,256]{3,2,1,0:T(8,128)(2,1)S(1)}, u32[]{:S(2)}, u32[]{:S(2)}) %all-to-all-start.1) | async-done | bytes 32800 | tf_op jit(solution)/shard_map/all_to_all | solution.py:129
  51.5 7.5 %while.98 = (s32[]{:T(128)}, f32[256,2,256]{2,0,1:T(8,128)}, bf16[4,256,256]{2,1,0:T(8,128)(2,1)S(1)}, f32[4,2,256]{2,1,0:T(2,128)S(1)}, bf16[4,256,256]{2,1,0:T(8,128)(2,1)S(1)}, /*index=5*/s32[]{:T(128)}, s32[]{:T(128)}) while((s32[]{:T(128)}, f32[256,2,256]{2,0,1:T(8,128)}, bf16[4,256,256]{2,1,0:T(8,128)(2,1)S(1)}, ...), condition=%wide.region_3.4_spmd.clone, body=%wide.region_2.3_spmd.clone.sunk | while | flops 67698688 | bytes 1841251 | solution.py:166
  52.7 2.1 convolution_add_fusion.8
  54.8 2.1 convolution_add_fusion.8
  57.0 2.1 convolution_add_fusion.8
  62.2 2.6 select_select_fusion
  66.3 22.6 %reduce-scatter.5.cloned.1.call-done = f32[32,2,256]{2,0,1:T(8,128)} async-done(((f32[256,2,256]{2,0,1:T(8,128)}), f32[32,2,256]{2,0,1:T(8,128)}) %reduce-scatter.5.cloned.1.call-update) | async-done | bytes 65552 | tf_op jit(solution)/shard_map/reduce_scatter | solution.py:211
  93.1 3.4 all-to-all-start.2
  98.1 4.3 all-to-all-done.2
  109.8 5.0 %all-gather = f32[64,2,256]{2,0,1:T(8,128)} all-gather(f32[32,2,256]{2,0,1:T(8,128)S(1)} %pad_maximum_fusion.12), channel_id=2, replica_groups=mesh['grp'=2,'tile'=4,'coil'=2,'spk'=2] {'coil'}, dimensions={0}, use_global_device_ids=true | all-gather | bytes 196608 | tf_op jit(solution)/shard_map/all_gather | solution.py:223
  122.1 4.0 all-to-all-start.3
  126.9 5.1 %all-to-all-done.3 = f32[8,1,2048]{2,1,0:T(1,128)} async-done(((f32[8,1,2048]{2,1,0:T(1,128)}), f32[8,1,2048]{2,1,0:T(1,128)}, u32[]{:S(2)}, u32[]{:S(2)}) %all-to-all-start.3) | async-done | bytes 65568 | tf_op jit(solution)/shard_map/all_to_all | solution.py:179
  132.0 2.3 reduce.1
  141.2 14.2 %all_gather.39 = bf16[256,2,256]{2,0,1:T(8,128)(2,1)S(1)} all-gather(bf16[32,2,256]{2,0,1:T(8,128)(2,1)S(1)} %fusion.32), channel_id=1, replica_groups=mesh['grp'=2,'tile'=4,'coil'=2,'spk'=2] {'tile','spk'}, dimensions={0}, use_global_device_ids=true | all-gather | bytes 294912 | tf_op jit(solution)/shard_map/all_gather | solution.py:185
  157.1 13.6 %while.95 = (s32[]{:T(128)}, f32[4,2,256]{2,1,0:T(2,128)}, bf16[4,256,256]{2,1,0:T(8,128)(2,1)S(1)}, bf16[512,256]{1,0:T(8,128)(2,1)}, bf16[4,256,256]{2,1,0:T(8,128)(2,1)S(1)}, /*index=5*/s32[]{:T(128)}) while((s32[]{:T(128)}, f32[4,2,256]{2,1,0:T(2,128)}, bf16[4,256,256]{2,1,0:T(8,128)(2,1)S(1)}, bf16[512,256]{1,0:T(8,128)(2,1)}, ...), condition=%wide.region_8.9_spmd, body=%wide.region_6.8_spmd.sunk | while | flops 67436544 | bytes 4203085 | solution.py:206
  172.1 7.5 %while.99 = (s32[]{:T(128)}, f32[256,2,256]{2,0,1:T(8,128)}, bf16[4,256,256]{2,1,0:T(8,128)(2,1)S(1)}, f32[4,2,256]{2,1,0:T(2,128)S(1)}, bf16[4,256,256]{2,1,0:T(8,128)(2,1)S(1)}, /*index=5*/s32[]{:T(128)}, s32[]{:T(128)}) while((s32[]{:T(128)}, f32[256,2,256]{2,0,1:T(8,128)}, bf16[4,256,256]{2,1,0:T(8,128)(2,1)S(1)}, ...), condition=%wide.region_10.11_spmd.clone, body=%wide.region_9.10_spmd.clone.sunk | while | flops 67698688 | bytes 1841251 | solution.py:166
  173.3 2.1 convolution_add_fusion.9
  175.4 2.1 convolution_add_fusion.9
  177.5 2.1 convolution_add_fusion.9
  179.7 29.8 %reduce-scatter.7.cloned.1.call-done = f32[32,2,256]{2,0,1:T(8,128)} async-done(((f32[256,2,256]{2,0,1:T(8,128)}), f32[32,2,256]{2,0,1:T(8,128)}) %reduce-scatter.7.cloned.1.call-update) | async-done | bytes 65552 | tf_op jit(solution)/shard_map/reduce_scatter | solution.py:211
  211.5 8.3 %all_to_all.136 = f32[8,1,2048]{2,1,0:T(1,128)S(1)} all-to-all(f32[8,1,2048]{2,1,0:T(1,128)S(1)} %reshape.890), channel_id=1, replica_groups=mesh['grp'=2,'tile'=4,'coil'=2,'spk'=2] {'tile','spk'}, dimensions={0} | all-to-all | bytes 131072 | tf_op jit(solution)/shard_map/all_to_all | solution.py:218
  221.9 4.9 %all-gather.1 = f32[64,2,256]{2,0,1:T(8,128)S(1)} all-gather(f32[32,2,256]{2,0,1:T(8,128)S(1)} %pad_maximum_fusion.13), channel_id=3, replica_groups=mesh['grp'=2,'tile'=4,'coil'=2,'spk'=2] {'coil'}, dimensions={0}, use_global_device_ids=true | all-gather | bytes 196608 | tf_op jit(solution)/shard_map/all_gather | solution.py:223
  233.5 4.0 all-to-all-start.5
  237.5 5.9 %all-to-all-done.5 = f32[8,1,2048]{2,1,0:T(1,128)} async-done(((f32[8,1,2048]{2,1,0:T(1,128)}), f32[8,1,2048]{2,1,0:T(1,128)}, u32[]{:S(2)}, u32[]{:S(2)}) %all-to-all-start.5) | async-done | bytes 65568 | tf_op jit(solution)/shard_map/all_to_all | solution.py:179
  243.4 2.3 reduce.3
  252.6 14.4 %all_gather.42 = bf16[256,2,256]{2,0,1:T(8,128)(2,1)S(1)} all-gather(bf16[32,2,256]{2,0,1:T(8,128)(2,1)S(1)} %fusion.33), channel_id=1, replica_groups=mesh['grp'=2,'tile'=4,'coil'=2,'spk'=2] {'tile','spk'}, dimensions={0}, use_global_device_ids=true | all-gather | bytes 294912 | tf_op jit(solution)/shard_map/all_gather | solution.py:185
  268.7 13.6 %while.96 = (s32[]{:T(128)}, f32[4,2,256]{2,1,0:T(2,128)}, bf16[4,256,256]{2,1,0:T(8,128)(2,1)S(1)}, bf16[512,256]{1,0:T(8,128)(2,1)}, bf16[4,256,256]{2,1,0:T(8,128)(2,1)S(1)}, /*index=5*/s32[]{:T(128)}) while((s32[]{:T(128)}, f32[4,2,256]{2,1,0:T(2,128)}, bf16[4,256,256]{2,1,0:T(8,128)(2,1)S(1)}, bf16[512,256]{1,0:T(8,128)(2,1)}, ...), condition=%wide.region_15.16_spmd, body=%wide.region_13.15_spmd.sunk | while | flops 67436544 | bytes 4203085 | solution.py:206
  283.7 7.5 %while.100 = (s32[]{:T(128)}, f32[256,2,256]{2,0,1:T(8,128)}, bf16[4,256,256]{2,1,0:T(8,128)(2,1)S(1)}, f32[4,2,256]{2,1,0:T(2,128)S(1)}, bf16[4,256,256]{2,1,0:T(8,128)(2,1)S(1)}, /*index=5*/s32[]{:T(128)}, s32[]{:T(128)}) while((s32[]{:T(128)}, f32[256,2,256]{2,0,1:T(8,128)}, bf16[4,256,256]{2,1,0:T(8,128)(2,1)S(1)}, ...), condition=%wide.region_17.18_spmd.clone, body=%wide.region_16.17_spmd.clone.sunk | while | flops 67698688 | bytes 1841251 | solution.py:166
  284.9 2.1 convolution_add_fusion.10
  287.0 2.1 convolution_add_fusion.10
  289.2 2.1 convolution_add_fusion.10
  291.3 29.9 %reduce-scatter.9.cloned.1.call-done = f32[32,2,256]{2,0,1:T(8,128)} async-done(((f32[256,2,256]{2,0,1:T(8,128)}), f32[32,2,256]{2,0,1:T(8,128)}) %reduce-scatter.9.cloned.1.call-update) | async-done | bytes 65552 | tf_op jit(solution)/shard_map/reduce_scatter | solution.py:211
  323.1 8.3 %all_to_all.137 = f32[8,1,2048]{2,1,0:T(1,128)S(1)} all-to-all(f32[8,1,2048]{2,1,0:T(1,128)S(1)} %reshape.894), channel_id=1, replica_groups=mesh['grp'=2,'tile'=4,'coil'=2,'spk'=2] {'tile','spk'}, dimensions={0} | all-to-all | bytes 131072 | tf_op jit(solution)/shard_map/all_to_all | solution.py:218
  333.6 4.9 %all-gather.2 = f32[64,2,256]{2,0,1:T(8,128)S(1)} all-gather(f32[32,2,256]{2,0,1:T(8,128)S(1)} %pad_maximum_fusion.14), channel_id=4, replica_groups=mesh['grp'=2,'tile'=4,'coil'=2,'spk'=2] {'coil'}, dimensions={0}, use_global_device_ids=true | all-gather | bytes 196608 | tf_op jit(solution)/shard_map/all_gather | solution.py:223
  345.2 4.0 all-to-all-start.7
  349.2 5.9 %all-to-all-done.7 = f32[8,1,2048]{2,1,0:T(1,128)} async-done(((f32[8,1,2048]{2,1,0:T(1,128)}), f32[8,1,2048]{2,1,0:T(1,128)}, u32[]{:S(2)}, u32[]{:S(2)}) %all-to-all-start.7) | async-done | bytes 65568 | tf_op jit(solution)/shard_map/all_to_all | solution.py:179
  355.1 2.3 reduce.5
  364.2 14.2 %all_gather.45 = bf16[256,2,256]{2,0,1:T(8,128)(2,1)S(1)} all-gather(bf16[32,2,256]{2,0,1:T(8,128)(2,1)S(1)} %fusion.34), channel_id=1, replica_groups=mesh['grp'=2,'tile'=4,'coil'=2,'spk'=2] {'tile','spk'}, dimensions={0}, use_global_device_ids=true | all-gather | bytes 294912 | tf_op jit(solution)/shard_map/all_gather | solution.py:185
  380.1 13.6 %while.97 = (s32[]{:T(128)}, f32[4,2,256]{2,1,0:T(2,128)}, bf16[4,256,256]{2,1,0:T(8,128)(2,1)S(1)}, bf16[512,256]{1,0:T(8,128)(2,1)}, bf16[4,256,256]{2,1,0:T(8,128)(2,1)S(1)}, /*index=5*/s32[]{:T(128)}) while((s32[]{:T(128)}, f32[4,2,256]{2,1,0:T(2,128)}, bf16[4,256,256]{2,1,0:T(8,128)(2,1)S(1)}, bf16[512,256]{1,0:T(8,128)(2,1)}, ...), condition=%wide.region_22.23_spmd, body=%wide.region_20.22_spmd.sunk | while | flops 67436544 | bytes 4203085 | solution.py:206
  395.2 7.5 %while.101 = (s32[]{:T(128)}, f32[256,2,256]{2,0,1:T(8,128)}, bf16[4,256,256]{2,1,0:T(8,128)(2,1)S(1)}, f32[4,2,256]{2,1,0:T(2,128)S(1)}, bf16[4,256,256]{2,1,0:T(8,128)(2,1)S(1)}, /*index=5*/s32[]{:T(128)}, s32[]{:T(128)}) while((s32[]{:T(128)}, f32[256,2,256]{2,0,1:T(8,128)}, bf16[4,256,256]{2,1,0:T(8,128)(2,1)S(1)}, ...), condition=%wide.region_24.25_spmd.clone, body=%wide.region_23.24_spmd.clone.sunk | while | flops 67698688 | bytes 1841251 | solution.py:166
  398.5 2.1 convolution_add_fusion.11
  400.6 2.1 convolution_add_fusion.11
  402.7 30.0 %reduce-scatter.11.cloned.1.call-done = f32[32,2,256]{2,0,1:T(8,128)} async-done(((f32[256,2,256]{2,0,1:T(8,128)}), f32[32,2,256]{2,0,1:T(8,128)}) %reduce-scatter.11.cloned.1.call-update) | async-done | bytes 65552 | tf_op jit(solution)/shard_map/reduce_scatter | solution.py:211
  434.7 8.3 %all_to_all.138 = f32[8,1,2048]{2,1,0:T(1,128)S(1)} all-to-all(f32[8,1,2048]{2,1,0:T(1,128)S(1)} %reshape.898), channel_id=1, replica_groups=mesh['grp'=2,'tile'=4,'coil'=2,'spk'=2] {'tile','spk'}, dimensions={0} | all-to-all | bytes 131072 | tf_op jit(solution)/shard_map/all_to_all | solution.py:218
  445.1 4.9 %all-gather.3 = f32[64,2,256]{2,0,1:T(8,128)S(1)} all-gather(f32[32,2,256]{2,0,1:T(8,128)S(1)} %pad_maximum_fusion.15), channel_id=5, replica_groups=mesh['grp'=2,'tile'=4,'coil'=2,'spk'=2] {'coil'}, dimensions={0}, use_global_device_ids=true | all-gather | bytes 196608 | tf_op jit(solution)/shard_map/all_gather | solution.py:223
  (360 shorter events, 150.5 us)
Async XLA Ops:
  6.5 14.8 %copy-start = (s32[8,256]{1,0:T(8,128)S(1)}, s32[8,256]{1,0:T(8,128)}, u32[]{:S(2)}) copy-start(s32[8,256]{1,0:T(8,128)} %param.23) | copy-start | bytes 24580
  7.2 0.7 copy-start.20
  22.5 15.5 %all-to-all-start = ((s32[8,1,256]{2,1,0:T(1,128)}), s32[8,1,256]{2,1,0:T(1,128)S(1)}, u32[]{:S(2)}, u32[]{:S(2)}) async-start(s32[8,1,256]{2,1,0:T(1,128)} %copy.118), calls=%async_computation | async-start | bytes 16384 | tf_op jit(solution)/shard_map/all_to_all | solution.py:132
  27.8 37.0 %copy-start.21 = (s32[8]{0:T(128)}, s32[8]{0:T(128)S(1)}, u32[]{:S(2)}) copy-start(s32[8]{0:T(128)S(1)} %get-tuple-element.881) | copy-start | bytes 100
  27.8 37.0 %copy-start.23 = (s32[8]{0:T(128)}, s32[8]{0:T(128)S(1)}, u32[]{:S(2)}) copy-start(s32[8]{0:T(128)S(1)} %get-tuple-element.882) | copy-start | bytes 100
  32.7 0.7 copy-start.14
  33.4 0.7 copy-start.19
  33.4 1.3 copy-start.18
  34.9 104.7 %copy-start.1 = (f32[1,256,2,256]{3,1,2,0:T(8,128)}, f32[1,256,2,256]{3,1,2,0:T(8,128)S(1)}, u32[]{:S(2)}) copy-start(f32[1,256,2,256]{3,1,2,0:T(8,128)S(1)} %get-tuple-element.829) | copy-start | bytes 1572868
  35.0 104.7 %copy-start.4 = (f32[1,256,2,256]{3,1,2,0:T(8,128)}, f32[1,256,2,256]{3,1,2,0:T(8,128)S(1)}, u32[]{:S(2)}) copy-start(f32[1,256,2,256]{3,1,2,0:T(8,128)S(1)} %get-tuple-element.834) | copy-start | bytes 1572868
  36.8 1.2 copy-start.13
  38.0 10.8 %all-to-all-start.1 = ((bf16[8,1,8,256]{3,2,1,0:T(8,128)(2,1)}), bf16[8,1,8,256]{3,2,1,0:T(8,128)(2,1)S(1)}, u32[]{:S(2)}, u32[]{:S(2)}) async-start(bf16[8,1,8,256]{3,2,1,0:T(8,128)(2,1)} %bitcast.26), calls=%async_computation.1 | async-start | bytes 65536 | tf_op jit(solution)/shard_map/all_to_all | solution.py:129
  43.0 45.9 %reduce-scatter.5.cloned.1.call-start = ((), (), s32[]{:S(2)}) async-start(), calls=%async_computation.13 | async-start | bytes 589824 | tf_op jit(solution)/shard_map/reduce_scatter | solution.py:211
  49.3 0.6 copy-start.12
  59.1 0.7 copy-start.28
  59.1 0.7 copy-start.31
  61.4 0.6 copy-start.26
  61.4 0.6 copy-start.27
  61.4 0.6 copy-start.30
  64.8 0.7 copy-start.29
  93.1 9.2 %all-to-all-start.2 = ((f32[8,1,2048]{2,1,0:T(1,128)}), f32[8,1,2048]{2,1,0:T(1,128)S(1)}, u32[]{:S(2)}, u32[]{:S(2)}) async-start(f32[8,1,2048]{2,1,0:T(1,128)} %reshape.886), calls=%async_computation.3 | async-start | bytes 131072 | tf_op jit(solution)/shard_map/all_to_all | solution.py:218
  96.5 0.7 copy-start.32
  96.5 0.7 copy-start.22
  96.5 0.7 copy-start.24
  96.5 0.7 copy-start.25
  102.3 0.6 copy-start.7
  115.9 0.7 copy-start.8
  122.1 9.9 %all-to-all-start.3 = ((f32[8,1,2048]{2,1,0:T(1,128)}), f32[8,1,2048]{2,1,0:T(1,128)}, u32[]{:S(2)}, u32[]{:S(2)}) async-start(f32[8,1,2048]{2,1,0:T(1,128)} %reshape.888), calls=%async_computation.4 | async-start | bytes 131072 | tf_op jit(solution)/shard_map/all_to_all | solution.py:179
  126.1 83.4 %reduce-scatter.7.cloned.1.call-start = ((), (), s32[]{:S(2)}) async-start(), calls=%async_computation.14 | async-start | bytes 589824 | tf_op jit(solution)/shard_map/reduce_scatter | solution.py:211
  170.7 0.7 copy-start.15
  226.8 0.7 copy-start.9
  227.1 1.1 copy-start.5
  227.5 1.1 copy-start.2
  233.5 9.9 %all-to-all-start.5 = ((f32[8,1,2048]{2,1,0:T(1,128)}), f32[8,1,2048]{2,1,0:T(1,128)}, u32[]{:S(2)}, u32[]{:S(2)}) async-start(f32[8,1,2048]{2,1,0:T(1,128)} %reshape.892), calls=%async_computation.7 | async-start | bytes 131072 | tf_op jit(solution)/shard_map/all_to_all | solution.py:179
  237.5 83.7 %reduce-scatter.9.cloned.1.call-start = ((), (), s32[]{:S(2)}) async-start(), calls=%async_computation.15 | async-start | bytes 589824 | tf_op jit(solution)/shard_map/reduce_scatter | solution.py:211
  282.3 0.7 copy-start.16
  338.5 0.7 copy-start.10
  338.7 1.1 copy-start.6
  339.2 1.1 copy-start.3
  345.2 9.9 %all-to-all-start.7 = ((f32[8,1,2048]{2,1,0:T(1,128)}), f32[8,1,2048]{2,1,0:T(1,128)}, u32[]{:S(2)}, u32[]{:S(2)}) async-start(f32[8,1,2048]{2,1,0:T(1,128)} %reshape.896), calls=%async_computation.10 | async-start | bytes 131072 | tf_op jit(solution)/shard_map/all_to_all | solution.py:179
  349.1 83.6 %reduce-scatter.11.cloned.1.call-start = ((), (), s32[]{:S(2)}) async-start(), calls=%async_computation.16 | async-start | bytes 589824 | tf_op jit(solution)/shard_map/reduce_scatter | solution.py:211
  393.8 0.7 copy-start.17
  450.2 0.7 copy-start.11
Sparse Core Ops, SparseCore 0:
  59.2 29.6 reduce-scatter.4
  179.8 29.6 reduce-scatter.6
  291.4 29.7 reduce-scatter.8
  402.8 29.8 reduce-scatter.10
